TPU v7x, 32 devices: a whole 2x2x4 slice. The times are simulated.
32 devices in a mesh: group: 8 (over z, y), peer: 4 (over x, core).
Axes of the slice: x: 2, y: 2, z: 4, core: 2. Of those that a mesh axis runs over, the one named last changes fastest.
Arguments:
- features: float32 [128, 64, 384], P('group', 'peer'), may hold values from -6 to 6
- image_of_row: int32 [8], replicated, may hold values from 0 to 3, never falling along the last dimension, each value on 1 to 4 neighbouring positions
- llm_peer: int32 [32, 1], P(('group', 'peer')), may hold values from 0 to 3, as said below
- token_grads: float32 [64, 64, 384], P(('group', 'peer')), may hold values from -6 to 6
- dw_weight: float32 [49, 384], replicated, may hold values from -0.875 to 0.875
- dw_bias: float32 [384], replicated, may hold values from -3 to 3
- ln_gain: float32 [384], replicated, may hold values from 0.1 to 1.9
- ln_bias: float32 [384], replicated, may hold values from -3 to 3
- w_in: bfloat16 [384, 1536], replicated, may hold values from -0.3125 to 0.3125
- b_in: float32 [1536], replicated, may hold values from -3 to 3
- w_out: bfloat16 [1536, 384], replicated, may hold values from -0.15625 to 0.15625
- b_out: float32 [384], replicated, may hold values from -3 to 3
- layer_scale: float32 [384], replicated, may hold values from 0.3 to 1
- comp_weight: bfloat16 [9, 384, 384], replicated, may hold values from -0.109375 to 0.109375
- comp_bias: float32 [384], replicated, may hold values from -3 to 3
Outputs:
- llm_tokens: float32 [64, 64, 384], P(('group', 'peer'))
- feature_grads: float32 [128, 64, 384], P('group', 'peer')
Inputs may be any that keep to these rules, and one draw needn't show every extreme that they name: `llm_peer`: the 1 tiles of one device go to 1 different peers of its group; each peer receives at most 2 tiles of its tile row, and in tile row 0 some peer receives exactly 2. `image_of_row`: Non-decreasing along tile rows; each image spans 1 to 4 consecutive tile rows.
All inputs are finite; a program needn't handle non-finite values.
Results may differ from a plain program's by a relative error of at most 0.005.
Values sent between devices are 32-bit elements; how exact they have to be, the bound alone decides.
A program may use at most 64 MiB of HBM per device.

v0:
```python
import jax
import jax.numpy as jnp
from jax import lax
from jax.sharding import PartitionSpec as P


def with_halo(cells, sides, width):
    for axis, dim in sides:
        count = lax.axis_size(axis)
        ends = count - 1
        head = lax.slice_in_dim(cells, 0, width, axis=dim)
        tail = lax.slice_in_dim(cells, cells.shape[dim] - width, cells.shape[dim], axis=dim)
        cells = jnp.concatenate(
            [
                lax.ppermute(tail, axis, [(i, (i + 1) % count) for i in range(ends)]),
                cells,
                lax.ppermute(head, axis, [((i + 1) % count, i) for i in range(ends)]),
            ],
            axis=dim,
        )
    return cells


def encode(tile_data, params):
    dw_weight, dw_bias, ln_gain, ln_bias, w_in, b_in, w_out, b_out, layer_scale = params
    tile_side = tile_data.shape[1]
    channels = tile_data.shape[3]
    padded = jnp.pad(tile_data, ((0, 0), (3, 3), (3, 3), (0, 0)))
    spatial = jnp.zeros_like(tile_data) + dw_bias
    for offset in range(49):
        row_off = offset // 7
        col_off = offset % 7
        spatial = (
            spatial
            + padded[:, row_off : row_off + tile_side, col_off : col_off + tile_side, :]
            * dw_weight[offset]
        )
    average = jnp.mean(spatial, axis=-1, keepdims=True)
    centered = spatial - average
    variance = jnp.mean(centered * centered, axis=-1, keepdims=True)
    normed = centered * lax.rsqrt(variance + 1e-06) * ln_gain + ln_bias
    flattened = normed.reshape(-1, channels).astype(jnp.bfloat16)
    hidden = jax.nn.gelu(
        jnp.dot(flattened, w_in, preferred_element_type=jnp.float32) + b_in, approximate=False
    )
    branch = jnp.dot(hidden.astype(jnp.bfloat16), w_out, preferred_element_type=jnp.float32) + b_out
    return tile_data + layer_scale * branch.reshape(tile_data.shape)


def pool_tiles(tile_data):
    tile_count, tile_side, other_side, channels = tile_data.shape
    return tile_data.reshape(tile_count, tile_side // 2, 2, other_side // 2, 2, channels).mean(
        axis=(2, 4)
    )


def spread_tiles(grad_data):
    return jnp.repeat(jnp.repeat(grad_data, 2, axis=1), 2, axis=2) * 0.25


def compress_conv(padded, kernel):
    out_rows = padded.shape[-3] - 2
    out_cols = padded.shape[-2] - 2
    leading = padded.shape[:-3]
    summed = jnp.zeros((1, kernel.shape[2]), jnp.float32)
    for offset in range(9):
        row_off = offset // 3
        col_off = offset % 3
        window = padded[..., row_off : row_off + out_rows, col_off : col_off + out_cols, :]
        window = window.reshape(-1, padded.shape[-1]).astype(jnp.bfloat16)
        summed = summed + jnp.dot(window, kernel[offset], preferred_element_type=jnp.float32)
    return summed.reshape(leading + (out_rows, out_cols, kernel.shape[2]))


def with_rims(pool_grid, keep_up, keep_down):
    padded = with_halo(pool_grid, (("group", 0), ("peer", 1)), 1)
    inner_rows = jnp.ones((pool_grid.shape[0],), jnp.float32)
    row_scale = jnp.concatenate([keep_up[None], inner_rows, keep_down[None]])
    return padded * row_scale[:, None, None]


def slot_table(all_peers, my_peer, peer_count, tile_count, slot_count):
    hits = (all_peers[:, 0].reshape(peer_count, tile_count) == my_peer).astype(jnp.float32)
    sends = jnp.sum(hits, axis=1)
    before = jnp.cumsum(sends) - sends
    slot_ids = jnp.arange(slot_count, dtype=jnp.int32).astype(jnp.float32)
    table = (before[None, :] == slot_ids[:, None]).astype(jnp.float32) * sends[None, :]
    return (hits, table)


def on_device(
    features,
    image_of_row,
    llm_peer,
    token_grads,
    dw_weight,
    dw_bias,
    ln_gain,
    ln_bias,
    w_in,
    b_in,
    w_out,
    b_out,
    layer_scale,
    comp_weight,
    comp_bias,
):
    params = (dw_weight, dw_bias, ln_gain, ln_bias, w_in, b_in, w_out, b_out, layer_scale)
    tile_side = features.shape[0]
    tile_count = features.shape[1] // tile_side
    channels = features.shape[2]
    half_side = tile_side // 2
    slot_count = token_grads.shape[0]
    peer_count = lax.axis_size("peer")
    group_count = lax.axis_size("group")
    group_index = lax.axis_index("group")
    my_peer = lax.axis_index("peer")

    def run_block(tile_data):
        return encode(tile_data, params)

    tile_data = features.reshape(tile_side, tile_count, tile_side, channels).transpose(1, 0, 2, 3)
    encoded = run_block(tile_data)
    pooled = pool_tiles(encoded)
    pool_grid = pooled.transpose(1, 0, 2, 3).reshape(half_side, tile_count * half_side, channels)
    own_image = image_of_row[group_index]
    image_above = image_of_row[jnp.maximum(group_index - 1, 0)]
    image_below = image_of_row[jnp.minimum(group_index + 1, group_count - 1)]
    keep_up = (image_above == own_image).astype(jnp.float32)
    keep_down = (image_below == own_image).astype(jnp.float32)
    compressed = compress_conv(with_rims(pool_grid, keep_up, keep_down), comp_weight) + comp_bias
    comp_tiles = compressed.reshape(half_side, tile_count, half_side, channels).transpose(
        1, 0, 2, 3
    )
    comp_tiles = comp_tiles.reshape(tile_count, half_side * half_side, channels)
    route_hot = (
        llm_peer[:, 0][:, None] == jnp.arange(peer_count, dtype=jnp.int32)[None, :]
    ).astype(jnp.float32)
    all_peers = lax.all_gather(llm_peer, "peer", axis=0, tiled=True)
    hits, table = slot_table(all_peers, my_peer, peer_count, tile_count, slot_count)
    outgoing = jnp.einsum("td,txc->dxc", route_hot, comp_tiles, precision=lax.Precision.HIGHEST)
    received = lax.all_to_all(outgoing, "peer", split_axis=0, concat_axis=0, tiled=True)
    llm_tokens = jnp.einsum("sp,pxc->sxc", table, received, precision=lax.Precision.HIGHEST)
    spread_back = jnp.einsum("sp,sxc->pxc", table, token_grads, precision=lax.Precision.HIGHEST)
    returned = lax.all_to_all(spread_back, "peer", split_axis=0, concat_axis=0, tiled=True)
    grad_tiles = jnp.einsum("td,dxc->txc", route_hot, returned, precision=lax.Precision.HIGHEST)
    grad_grid = grad_tiles.reshape(tile_count, half_side, half_side, channels).transpose(1, 0, 2, 3)
    grad_grid = grad_grid.reshape(half_side, tile_count * half_side, channels)
    flipped = jnp.transpose(comp_weight[::-1], (0, 2, 1))
    grad_pooled = compress_conv(with_rims(grad_grid, keep_up, keep_down), flipped)
    grad_pooled = grad_pooled.reshape(half_side, tile_count, half_side, channels).transpose(
        1, 0, 2, 3
    )
    grad_encoded = spread_tiles(grad_pooled)
    recomputed, pullback = jax.vjp(run_block, tile_data)
    grad_input = pullback(grad_encoded)[0]
    feature_grads = grad_input.transpose(1, 0, 2, 3).reshape(
        tile_side, tile_count * tile_side, channels
    )
    return (llm_tokens, feature_grads)


def solution(mesh):
    placed = (
        P("group", "peer", None),
        P(),
        P(("group", "peer"), None),
        P(("group", "peer"), None, None),
        P(),
        P(),
        P(),
        P(),
        P(),
        P(),
        P(),
        P(),
        P(),
        P(),
        P(),
    )
    return jax.shard_map(
        on_device,
        mesh=mesh,
        in_specs=placed,
        out_specs=(P(("group", "peer"), None, None), P("group", "peer", None)),
        check_vma=False,
    )
```

profile of v0, /device:TPU:25, one launch (start us, length us, event | category | flops | bytes accessed | tf_op | source)
XLA Modules:
  0.0 116.1 jit_solution(4482224627716709767)
XLA Ops:
  1.8 1.2 %slice_reduce_fusion.47 = (f32[384]{0:T(512)S(1)}, f32[384]{0:T(512)S(1)}, f32[384]{0:T(512)S(1)}, f32[384]{0:T(512)S(1)}, f32[384]{0:T(512)S(1)}, /*index=5*/f3...) fusion(f32[49,384]{1,0:T(8,128)} %param.19), kind=kLoop, calls=%fused_computation.397 | loop fusion | bytes 58368 | tf_op jit(solution)/shard_map/slice | solution.py:36
  4.0 15.1 %fusion.183 = (f32[16,16]{1,0:T(8,128)S(1)}, f32[1,16,16,384]{3,2,1,0:T(8,128)S(1)}) fusion(f32[384]{0:T(512)S(1)} %get-tuple-element.53, f32[384]{0:T(512)S(1)} %get-tuple-element.54, f32[384]{0:T(512)S(1)} %get-tuple-element.7, f32[384]{0:T(512)S(1)} %get-tuple-element.8, f32[384]{0:T(512)S(1)} %get-tuple-element.9, f32[384]{0:T(512)S(1)} %get-tuple-element.10, ...), kind=kLoop, calls=%fused_computation.422 | loop fusion | flops 9731840 | bytes 1257472 | tf_op jit(solution)/shard_map/reduce_sum | solution.py:38
  19.5 4.2 %fusion.1 = (f32[256,1536]{1,0:T(8,128)S(1)}, f32[256,1536]{1,0:T(8,128)S(1)}) fusion(f32[1536]{0:T(1024)S(1)} %copy-done.14, bf16[256,384]{1,0:T(8,128)(2,1)S(1)} %bitcast.174, bf16[384,1536]{1,0:T(8,128)(2,1)S(1)} %copy-done), kind=kOutput, calls=%fused_computation.53 | convolution fusion | flops 326762496 | bytes 4528128 | tf_op jit(solution)/shard_map/dot_general | solution.py:44
  26.1 3.1 %collective-permute-start = (f32[1,8,384]{2,1,0:T(8,128)S(1)}, f32[1,8,384]{2,1,0:T(8,128)S(1)}, u32[]{:S(2)}, u32[]{:S(2)}) collective-permute-start(f32[1,8,384]{2,1,0:T(8,128)S(1)} %get-tuple-element.115), channel_id=1, source_target_pairs={{0,4},{4,8},{8,12},{12,16},{16,20},{20,24},{24,28},{1,5},{5,9},{9,... | collective-permute-start | bytes 36872 | tf_op jit(solution)/shard_map/ppermute | solution.py:15
  31.2 3.0 %collective-permute-start.1 = (f32[1,8,384]{2,1,0:T(8,128)S(1)}, f32[1,8,384]{2,1,0:T(8,128)S(1)}, u32[]{:S(2)}, u32[]{:S(2)}) collective-permute-start(f32[1,8,384]{2,1,0:T(8,128)S(1)} %get-tuple-element.116), channel_id=1, source_target_pairs={{4,0},{8,4},{12,8},{16,12},{20,16},{24,20},{28,24},{5,1},{9,5},{13... | collective-permute-start | bytes 36872 | tf_op jit(solution)/shard_map/ppermute | solution.py:17
  34.2 4.8 %all-reduce.50 = s32[4]{0:T(128)S(1)} all-reduce(s32[4]{0:T(128)S(1)} %bitcast_dynamic-update-slice_fusion), channel_id=1, replica_groups=mesh['group'=8,'peer'=4] {'peer'}, use_global_device_ids=true, to_apply=%add.50 | all-reduce | flops 4 | bytes 32
  41.1 4.8 %all-to-all-start.1 = ((f32[4,64,384]{2,1,0:T(8,128)}), f32[4,64,384]{2,1,0:T(8,128)S(1)}, u32[]{:S(2)}, u32[]{:S(2)}) async-start(f32[4,64,384]{2,1,0:T(8,128)} %copy.21), calls=%async_computation.1 | async-start | bytes 786432 | tf_op jit(solution)/shard_map/all_to_all | solution.py:145
  49.0 3.6 %reverse_bitcast_fusion = bf16[9,384,384]{1,2,0:T(8,128)(2,1)} fusion(bf16[9,384,384]{2,1,0:T(8,128)(2,1)} %param.28), kind=kLoop, calls=%fused_computation.49 | loop fusion | bytes 5308416 | tf_op jit(solution)/shard_map/transpose | solution.py:149
  53.3 2.4 %collective-permute-start.4 = (f32[1,8,384]{2,1,0:T(8,128)S(1)}, f32[1,8,384]{2,1,0:T(8,128)S(1)}, u32[]{:S(2)}, u32[]{:S(2)}) collective-permute-start(f32[1,8,384]{2,1,0:T(8,128)S(1)} %get-tuple-element.111), channel_id=1, source_target_pairs={{0,4},{4,8},{8,12},{12,16},{16,20},{20,24},{24,28},{1,5},{5,9},{9,... | collective-permute-start | bytes 36872 | tf_op jit(solution)/shard_map/ppermute | solution.py:15
  55.7 3.9 %collective-permute-start.5 = (f32[1,8,384]{2,1,0:T(8,128)S(1)}, f32[1,8,384]{2,1,0:T(8,128)S(1)}, u32[]{:S(2)}, u32[]{:S(2)}) collective-permute-start(f32[1,8,384]{2,1,0:T(8,128)S(1)} %get-tuple-element.112), channel_id=1, source_target_pairs={{4,0},{8,4},{12,8},{16,12},{20,16},{24,20},{28,24},{5,1},{9,5},{13... | collective-permute-start | bytes 36872 | tf_op jit(solution)/shard_map/ppermute | solution.py:17
  59.7 4.1 %collective-permute-start.2 = (f32[10,1,384]{2,1,0:T(1,128)S(1)}, f32[10,1,384]{2,1,0:T(1,128)S(1)}, u32[]{:S(2)}, u32[]{:S(2)}) collective-permute-start(f32[10,1,384]{2,1,0:T(1,128)S(1)} %get-tuple-element.109), channel_id=1, source_target_pairs={{0,1},{1,2},{2,3},{4,5},{5,6},{6,7},{8,9},{9,10},{10,11},{12,13},{... | collective-permute-start | bytes 46088 | tf_op jit(solution)/shard_map/ppermute | solution.py:15
  63.8 1.9 %collective-permute-start.3 = (f32[10,1,384]{2,1,0:T(1,128)S(1)}, f32[10,1,384]{2,1,0:T(1,128)S(1)}, u32[]{:S(2)}, u32[]{:S(2)}) collective-permute-start(f32[10,1,384]{2,1,0:T(1,128)S(1)} %get-tuple-element.110), channel_id=1, source_target_pairs={{1,0},{2,1},{3,2},{5,4},{6,5},{7,6},{9,8},{10,9},{11,10},{13,12},{... | collective-permute-start | bytes 46088 | tf_op jit(solution)/shard_map/ppermute | solution.py:17
  65.8 3.6 %collective-permute-start.6 = (f32[10,1,384]{2,1,0:T(1,128)S(1)}, f32[10,1,384]{2,1,0:T(1,128)S(1)}, u32[]{:S(2)}, u32[]{:S(2)}) collective-permute-start(f32[10,1,384]{2,1,0:T(1,128)S(1)} %get-tuple-element.107), channel_id=1, source_target_pairs={{0,1},{1,2},{2,3},{4,5},{5,6},{6,7},{8,9},{9,10},{10,11},{12,13},{... | collective-permute-start | bytes 46088 | tf_op jit(solution)/shard_map/ppermute | solution.py:15
  69.4 2.1 %collective-permute-start.7 = (f32[10,1,384]{2,1,0:T(1,128)S(1)}, f32[10,1,384]{2,1,0:T(1,128)S(1)}, u32[]{:S(2)}, u32[]{:S(2)}) collective-permute-start(f32[10,1,384]{2,1,0:T(1,128)S(1)} %get-tuple-element.108), channel_id=1, source_target_pairs={{1,0},{2,1},{3,2},{5,4},{6,5},{7,6},{9,8},{10,9},{11,10},{13,12},{... | collective-permute-start | bytes 46088 | tf_op jit(solution)/shard_map/ppermute | solution.py:17
  71.6 2.8 %collective-permute-done.7 = f32[10,1,384]{2,1,0:T(1,128)S(1)} collective-permute-done((f32[10,1,384]{2,1,0:T(1,128)S(1)}, f32[10,1,384]{2,1,0:T(1,128)S(1)}, u32[]{:S(2)}, u32[]{:S(2)}) %collective-permute-start.7) | collective-permute-done | bytes 15392 | tf_op jit(solution)/shard_map/ppermute | solution.py:17
  80.0 3.6 %fusion.18 = bf16[256,384]{1,0:T(8,128)(2,1)S(1)} fusion(bf16[384,1536]{1,0:T(8,128)(2,1)S(1)} %copy-done, f32[256,1536]{1,0:T(8,128)} %copy-done.4, bf16[1536,384]{1,0:T(8,128)(2,1)} %param.25, f32[256,1536]{1,0:T(8,128)} %copy-done.5, f32[256,384]{1,0:T(8,128)S(1)} %broadcast_in_dim.18, f32[384]{0:T(512)S(1)} %broadcast_multiply_fusion.52), kind=kOutput, calls=%fused_computation.80 | convolution fusion | flops 610074624 | bytes 6096384 | tf_op jit(solution)/shard_map/transpose(jvp())/dot_general | solution.py:44
  85.1 3.0 %broadcast_multiply_fusion.4 = (f32[1,16,16,384]{3,2,1,0:T(8,128)}, f32[1,16,16,384]{3,2,1,0:T(8,128)}, f32[1,16,16,384]{3,2,1,0:T(8,128)}, f32[1,16,16,384]{3,2...) fusion(f32[1,16,16,384]{3,2,1,0:T(8,128)S(1)} %get-tuple-elemen, ...), kind=kLoop, calls=%fused_computation.263 | loop fusion | flops 1769472 | bytes 7498752 | tf_op jit(solution)/shard_map/transpose(jvp())/mul | solution.py:35
  88.0 2.5 %broadcast_multiply_fusion.3 = (f32[1,16,16,384]{3,2,1,0:T(8,128)}, f32[1,16,16,384]{3,2,1,0:T(8,128)S(1)}, f32[1,16,16,384]{3,2,1,0:T(8,128)S(1)}, f32[1,16,16,...) fusion(f32[1,16,16,384]{3,2,1,0:T(8,128)S(1)} %get-tuple-elemen, ...), kind=kLoop, calls=%fused_computation.262 | loop fusion | flops 1769472 | bytes 7498752 | tf_op jit(solution)/shard_map/transpose(jvp())/mul | solution.py:35
  90.6 2.4 %broadcast_multiply_fusion.5 = (f32[1,16,16,384]{3,2,1,0:T(8,128)}, f32[1,16,16,384]{3,2,1,0:T(8,128)}, f32[1,16,16,384]{3,2,1,0:T(8,128)}, f32[1,16,16,384]{3,2...) fusion(f32[1,16,16,384]{3,2,1,0:T(8,128)S(1)} %get-tuple-elemen, ...), kind=kLoop, calls=%fused_computation.264 | loop fusion | flops 1179648 | bytes 5130240 | tf_op jit(solution)/shard_map/transpose(jvp())/mul | solution.py:35
  96.6 4.1 %all-to-all-start = ((f32[4,64,384]{2,1,0:T(8,128)}), f32[4,64,384]{2,1,0:T(8,128)}, u32[]{:S(2)}, u32[]{:S(2)}) async-start(f32[4,64,384]{2,1,0:T(8,128)} %broadcast_multiply_fusion.1), calls=%async_computation | async-start | bytes 786432 | tf_op jit(solution)/shard_map/all_to_all | solution.py:142
  100.7 7.6 %pad_add_fusion = f32[1,22,22,384]{3,2,1,0:T(8,128)S(1)} fusion(f32[1,16,16,384]{3,2,1,0:T(8,128)} %get-tuple-element.65, f32[1,16,16,384]{3,2,1,0:T(8,128)} %get-tuple-element.66, f32[1,16,16,384]{3,2,1,0:T(8,128)} %get-tuple-element.67, f32[1,16,16,384]{3,2,1,0:T(8,128)} %get-tuple-element.68, f32[1,16,16,384]{3,2,1,0:T(8,128)} %get-tuple-element.69, ...), kind=kLoop, calls=%fused_computation.99 | loop fusion | flops 7805952 | bytes 17651712 | tf_op jit(solution)/shard_map/transpose(jvp())/add_any | solution.py:35
  109.1 2.0 %mul.1330 = f32[1,16,16,384]{3,2,1,0:T(8,128)} reshape(f32[16,8,2,384]{3,2,1,0:T(2,128)} %broadcast_in_dim.16) | data formatting | bytes 786432 | tf_op jit(solution)/shard_map/mul | solution.py:58
  111.2 2.2 %fusion.125 = f32[16,16,384]{2,1,0:T(8,128)} fusion(f32[1,16,16,384]{3,2,1,0:T(8,128)} %mul.1330, f32[1,16,16,384]{3,2,1,0:T(8,128)} %get-tuple-element.106, f32[1,16,16,384]{3,2,1,0:T(8,128)S(1)} %get-tuple-element.60, f32[1,16,16,384]{3,2,1,0:T(8,128)S(1)} %get-tuple-element.61, f32[1,16,16,384]{3,2,1,0:T(8,128)S(1)} %get-tuple-element.62, ...), kind=kLoop, calls=%fused_computation.204 | loop fusion | flops 688128 | bytes 3538944 | tf_op jit(solution)/shard_map/reshape;transpose | solution.py:157
  113.4 2.0 %fusion.131 = f32[2,64,384]{2,0,1:T(2,128)S(1)} fusion(f32[4,64,384]{2,1,0:T(8,128)} %all-to-all-done, f32[4]{0:T(128)S(1)} %compare_convert_fusion, f32[4]{0:T(128)S(1)} %bitcast_subtract_fusion, f32[2]{0:T(128)S(1)} %iota_convert_fusion), kind=kOutput, calls=%fused_computation.216 | convolution fusion | flops 2359312 | bytes 589864 | tf_op jit(solution)/shard_map/sp,pxc->sxc/dot_general | solution.py:143
  (104 shorter events, 21.6 us)
Async XLA Ops:
  0.6 18.9 %copy-start = (bf16[384,1536]{1,0:T(8,128)(2,1)S(1)}, bf16[384,1536]{1,0:T(8,128)(2,1)}, u32[]{:S(2)}) copy-start(bf16[384,1536]{1,0:T(8,128)(2,1)} %param.23) | copy-start | bytes 3538948
  0.6 18.7 %copy-start.8 = (f32[384]{0:T(512)S(1)}, f32[384]{0:T(512)}, u32[]{:S(2)}) copy-start(f32[384]{0:T(512)} %param.21) | copy-start | bytes 4612
  0.7 18.7 %copy-start.11 = (f32[384]{0:T(512)S(1)}, f32[384]{0:T(512)}, u32[]{:S(2)}) copy-start(f32[384]{0:T(512)} %param.22) | copy-start | bytes 4612
  0.7 18.9 %copy-start.14 = (f32[1536]{0:T(1024)S(1)}, f32[1536]{0:T(1024)}, u32[]{:S(2)}) copy-start(f32[1536]{0:T(1024)} %param.24) | copy-start | bytes 18436
  19.5 4.3 %copy-start.6 = (bf16[1536,384]{1,0:T(8,128)(2,1)S(1)}, bf16[1536,384]{1,0:T(8,128)(2,1)}, u32[]{:S(2)}) copy-start(bf16[1536,384]{1,0:T(8,128)(2,1)} %param.25) | copy-start | bytes 3538948
  19.5 4.2 %copy-start.12 = (f32[384]{0:T(512)S(1)}, f32[384]{0:T(512)}, u32[]{:S(2)}) copy-start(f32[384]{0:T(512)} %param.26) | copy-start | bytes 4612
  23.8 1.7 %copy-start.5 = (f32[256,1536]{1,0:T(8,128)}, f32[256,1536]{1,0:T(8,128)S(1)}, u32[]{:S(2)}) copy-start(f32[256,1536]{1,0:T(8,128)S(1)} %get-tuple-element.125) | copy-start | bytes 4718596
  23.8 1.7 %copy-start.3 = (f32[16,16,384]{2,1,0:T(8,128)S(1)}, f32[16,16,384]{2,1,0:T(8,128)}, u32[]{:S(2)}) copy-start(f32[16,16,384]{2,1,0:T(8,128)} %param.15) | copy-start | bytes 1179652
  23.8 1.7 %copy-start.9 = (f32[384]{0:T(512)S(1)}, f32[384]{0:T(512)}, u32[]{:S(2)}) copy-start(f32[384]{0:T(512)} %param.27) | copy-start | bytes 4612
  25.5 4.4 %copy-start.15 = (u32[32]{0:T(128)S(1)}, u32[32]{0:T(128)}, u32[]{:S(2)}) copy-start(u32[32]{0:T(128)} %constant.209) | copy-start | bytes 388
  25.5 13.8 %copy-start.7 = (f32[2,64,384]{2,1,0:T(8,128)S(1)}, f32[2,64,384]{2,1,0:T(8,128)}, u32[]{:S(2)}) copy-start(f32[2,64,384]{2,1,0:T(8,128)} %param.18) | copy-start | bytes 589828
  25.8 20.1 %copy-start.10 = (s32[8]{0:T(128)S(1)}, s32[8]{0:T(128)}, u32[]{:S(2)}) copy-start(s32[8]{0:T(128)} %param.16) | copy-start | bytes 100
  26.1 33.6 %collective-permute-start = (f32[1,8,384]{2,1,0:T(8,128)S(1)}, f32[1,8,384]{2,1,0:T(8,128)S(1)}, u32[]{:S(2)}, u32[]{:S(2)}) collective-permute-start(f32[1,8,384]{2,1,0:T(8,128)S(1)} %get-tuple-element.115), channel_id=1, source_target_pairs={{0,4},{4,8},{8,12},{12,16},{16,20},{20,24},{24,28},{1,5},{5,9},{9,... | collective-permute-start | bytes 36872 | tf_op jit(solution)/shard_map/ppermute | solution.py:15
  31.2 28.5 %collective-permute-start.1 = (f32[1,8,384]{2,1,0:T(8,128)S(1)}, f32[1,8,384]{2,1,0:T(8,128)S(1)}, u32[]{:S(2)}, u32[]{:S(2)}) collective-permute-start(f32[1,8,384]{2,1,0:T(8,128)S(1)} %get-tuple-element.116), channel_id=1, source_target_pairs={{4,0},{8,4},{12,8},{16,12},{20,16},{24,20},{28,24},{5,1},{9,5},{13... | collective-permute-start | bytes 36872 | tf_op jit(solution)/shard_map/ppermute | solution.py:17
  41.1 11.5 %all-to-all-start.1 = ((f32[4,64,384]{2,1,0:T(8,128)}), f32[4,64,384]{2,1,0:T(8,128)S(1)}, u32[]{:S(2)}, u32[]{:S(2)}) async-start(f32[4,64,384]{2,1,0:T(8,128)} %copy.21), calls=%async_computation.1 | async-start | bytes 786432 | tf_op jit(solution)/shard_map/all_to_all | solution.py:145
  52.6 25.6 %copy-start.2 = (bf16[9,384,384]{1,2,0:T(8,128)(2,1)S(1)}, bf16[9,384,384]{1,2,0:T(8,128)(2,1)}, u32[]{:S(2)}) copy-start(bf16[9,384,384]{1,2,0:T(8,128)(2,1)} %reverse_bitcast_fusion) | copy-start | bytes 7962628
  53.3 12.4 %collective-permute-start.4 = (f32[1,8,384]{2,1,0:T(8,128)S(1)}, f32[1,8,384]{2,1,0:T(8,128)S(1)}, u32[]{:S(2)}, u32[]{:S(2)}) collective-permute-start(f32[1,8,384]{2,1,0:T(8,128)S(1)} %get-tuple-element.111), channel_id=1, source_target_pairs={{0,4},{4,8},{8,12},{12,16},{16,20},{20,24},{24,28},{1,5},{5,9},{9,... | collective-permute-start | bytes 36872 | tf_op jit(solution)/shard_map/ppermute | solution.py:15
  55.7 10.0 %collective-permute-start.5 = (f32[1,8,384]{2,1,0:T(8,128)S(1)}, f32[1,8,384]{2,1,0:T(8,128)S(1)}, u32[]{:S(2)}, u32[]{:S(2)}) collective-permute-start(f32[1,8,384]{2,1,0:T(8,128)S(1)} %get-tuple-element.112), channel_id=1, source_target_pairs={{4,0},{8,4},{12,8},{16,12},{20,16},{24,20},{28,24},{5,1},{9,5},{13... | collective-permute-start | bytes 36872 | tf_op jit(solution)/shard_map/ppermute | solution.py:17
  59.7 11.9 %collective-permute-start.2 = (f32[10,1,384]{2,1,0:T(1,128)S(1)}, f32[10,1,384]{2,1,0:T(1,128)S(1)}, u32[]{:S(2)}, u32[]{:S(2)}) collective-permute-start(f32[10,1,384]{2,1,0:T(1,128)S(1)} %get-tuple-element.109), channel_id=1, source_target_pairs={{0,1},{1,2},{2,3},{4,5},{5,6},{6,7},{8,9},{9,10},{10,11},{12,13},{... | collective-permute-start | bytes 46088 | tf_op jit(solution)/shard_map/ppermute | solution.py:15
  63.8 7.8 %collective-permute-start.3 = (f32[10,1,384]{2,1,0:T(1,128)S(1)}, f32[10,1,384]{2,1,0:T(1,128)S(1)}, u32[]{:S(2)}, u32[]{:S(2)}) collective-permute-start(f32[10,1,384]{2,1,0:T(1,128)S(1)} %get-tuple-element.110), channel_id=1, source_target_pairs={{1,0},{2,1},{3,2},{5,4},{6,5},{7,6},{9,8},{10,9},{11,10},{13,12},{... | collective-permute-start | bytes 46088 | tf_op jit(solution)/shard_map/ppermute | solution.py:17
  65.8 5.9 %collective-permute-start.6 = (f32[10,1,384]{2,1,0:T(1,128)S(1)}, f32[10,1,384]{2,1,0:T(1,128)S(1)}, u32[]{:S(2)}, u32[]{:S(2)}) collective-permute-start(f32[10,1,384]{2,1,0:T(1,128)S(1)} %get-tuple-element.107), channel_id=1, source_target_pairs={{0,1},{1,2},{2,3},{4,5},{5,6},{6,7},{8,9},{9,10},{10,11},{12,13},{... | collective-permute-start | bytes 46088 | tf_op jit(solution)/shard_map/ppermute | solution.py:15
  69.4 5.0 %collective-permute-start.7 = (f32[10,1,384]{2,1,0:T(1,128)S(1)}, f32[10,1,384]{2,1,0:T(1,128)S(1)}, u32[]{:S(2)}, u32[]{:S(2)}) collective-permute-start(f32[10,1,384]{2,1,0:T(1,128)S(1)} %get-tuple-element.108), channel_id=1, source_target_pairs={{1,0},{2,1},{3,2},{5,4},{6,5},{7,6},{9,8},{10,9},{11,10},{13,12},{... | collective-permute-start | bytes 46088 | tf_op jit(solution)/shard_map/ppermute | solution.py:17
  90.6 3.4 %copy-start.1 = (bf16[9,384,384]{2,1,0:T(8,128)(2,1)S(1)}, bf16[9,384,384]{2,1,0:T(8,128)(2,1)}, u32[]{:S(2)}) copy-start(bf16[9,384,384]{2,1,0:T(8,128)(2,1)} %param.28) | copy-start | bytes 7962628
  96.6 16.9 %all-to-all-start = ((f32[4,64,384]{2,1,0:T(8,128)}), f32[4,64,384]{2,1,0:T(8,128)}, u32[]{:S(2)}, u32[]{:S(2)}) async-start(f32[4,64,384]{2,1,0:T(8,128)} %broadcast_multiply_fusion.1), calls=%async_computation | async-start | bytes 786432 | tf_op jit(solution)/shard_map/all_to_all | solution.py:142
  (2 other events, 2.3 us)
where the time goes:
time: 117 us; the launch traced here: 116 us
  other arithmetic  36.2 us (31%)
  starting transfers between devices  33.1 us (28%)
  matrix products  18.7 us (16%)
  local copies, waits for them, and re-layouts  16 us (14%)
  blocking collectives  4.82 us (4%)
  between operations  4.37 us (4%)
  waiting for transfers between devices  2.86 us (2%)
    reduce_sum x1, other arithmetic, encode(): average = jnp.mean(spatial, axis=-1, keepdims=True)  15.1 us
    ppermute x4, starting transfers between devices, with_halo(): lax.ppermute(tail, axis, [(i, (i + 1) % count) for i in range(ends)])  13.3 us
    ppermute x4, starting transfers between devices, with_halo(): lax.ppermute(head, axis, [((i + 1) % count, i) for i in range(ends)])  11 us
    mul x4, other arithmetic, encode(): padded[:, row_off:row_off + tile_side, col_off:col_off + tile_side, :]  8.87 us
    dot_general x2, matrix products, encode(): jnp.dot(flattened, w_in, preferred_element_type=jnp.float32) + b_in  7.78 us
    add_any x1, other arithmetic, encode(): padded[:, row_off:row_off + tile_side, col_off:col_off + tile_side, :]  7.57 us
    dot_general x18, matrix products, compress_conv(): jnp.dot(window, kernel[offset], preferred_element_type=jnp.float32)  6.58 us
    unnamed x1, blocking collectives  4.82 us
  transfers between devices with their start and end apart: 10, of which 1 were waited for; matrix products, arithmetic and copies ran while one was open for 18% of the time, Pallas kernels for 0%

commit v1 on v0

v1 whole, which is shorter than its diff:
```python
import functools
import math

import jax
import jax.numpy as jnp
from jax import lax
from jax.experimental import pallas as pl
from jax.experimental.pallas import tpu as pltpu
from jax.sharding import PartitionSpec as P

MESH = pl.DeviceIdType.MESH
LANES = 128
PAD = 8
BLOCK = 256
ROWS = ((-1, -1), (-1, 0), (-1, 1), (0, -1), (0, 1), (1, -1), (1, 0), (1, 1))


def nt_dot(a, b):
    return lax.dot_general(a, b, (((1,), (1,)), ((), ())), preferred_element_type=jnp.float32)


def depthwise(src, weight, chunk, taps, side, flip):
    half = side // 2
    reach = taps // 2
    outs = []
    for parity in range(2):
        total = None
        for b in range(taps):
            rows = src[chunk, :, pl.ds(PAD - reach + parity + b, half, stride=2), :]
            for a in range(taps):
                k = (taps - 1 - a) * taps + taps - 1 - b if flip else a * taps + b
                term = rows[a : a + side] * weight[chunk, k : k + 1, :]
                total = term if total is None else total + term
        outs.append(total)
    return outs


def kernel(
    groups,
    peers,
    taps,
    image_hbm,
    owner_hbm,
    x_hbm,
    tg_hbm,
    dww_hbm,
    dwb_hbm,
    gain_hbm,
    lnb_hbm,
    win_hbm,
    bin_hbm,
    wout_hbm,
    bout_hbm,
    scale_hbm,
    cw_hbm,
    cb_hbm,
    tok_hbm,
    dx_hbm,
    xpad,
    gpad,
    dww,
    dwb,
    gain,
    lnb,
    bout,
    scale,
    cb,
    bin_,
    win,
    wout,
    cw,
    tg,
    sp,
    rstd,
    nb,
    dg,
    hb,
    dpb,
    table,
    sendg,
    recvg,
    tok,
    recvt,
    tokout,
    grid_g,
    grid_p,
    col_g,
    col_p,
    halo_g,
    halo_p,
    gq,
    obuf,
    image_ref,
    owner_ref,
    in_sems,
    out_sems,
    tab_send,
    tab_recv,
    g_send,
    g_recv,
    t_send,
    t_recv,
    hg_send,
    hg_recv,
    hp_send,
    hp_recv,
):
    g = lax.axis_index("group")
    me = lax.axis_index("peer")
    side = x_hbm.shape[0]
    channels = x_hbm.shape[2]
    half = side // 2
    cells = half * half
    chunks = channels // LANES
    reach = taps // 2
    hid = win.shape[1]
    slots = tg.shape[0]
    small = (dwb, gain, lnb, bout, scale, cb)

    def vector(ref, lane=slice(None)):
        return ref[lane].reshape(1, -1)

    halo_g[...] = jnp.zeros_like(halo_g)
    halo_p[...] = jnp.zeros_like(halo_p)
    barrier = pltpu.get_barrier_semaphore()

    def there(dr, dp):
        conds = []
        if dr < 0:
            conds.append(g > 0)
        if dr > 0:
            conds.append(g < groups - 1)
        if dp < 0:
            conds.append(me > 0)
        if dp > 0:
            conds.append(me < peers - 1)
        cond = conds[0]
        for other in conds[1:]:
            cond = jnp.logical_and(cond, other)
        return cond

    for k in range(1, peers):
        pl.semaphore_signal(
            barrier, inc=1, device_id={"group": g, "peer": lax.rem(me + k, peers)}, device_id_type=MESH
        )
    for dr, dp in ROWS:
        if dr != 0:

            @pl.when(there(dr, dp))
            def _():
                pl.semaphore_signal(
                    barrier, inc=1, device_id={"group": g + dr, "peer": me + dp}, device_id_type=MESH
                )

    copies = {}

    def fetch(name, src, dst):
        copy = pltpu.make_async_copy(src, dst, in_sems.at[len(copies)])
        copy.start()
        copies[name] = copy

    fetch("owner", owner_hbm, owner_ref)
    for c in range(chunks):
        lane = slice(c * LANES, (c + 1) * LANES)
        fetch(("w", c), dww_hbm.at[:, lane], dww.at[c])
        fetch(("x", c), x_hbm.at[:, :, lane], xpad.at[c, reach : reach + side, PAD : PAD + side, :])
    for i, src in enumerate((dwb_hbm, gain_hbm, lnb_hbm, bout_hbm, scale_hbm, cb_hbm)):
        fetch(("s", i), src, small[i])
    fetch("tg", tg_hbm, tg)
    fetch("image", image_hbm, image_ref)
    fetch("bin", bin_hbm, bin_)
    fetch("win", win_hbm, win)
    fetch("wout", wout_hbm, wout)
    fetch("cw", cw_hbm, cw)

    def clear(buf):
        width = buf.shape[2]
        for c in range(chunks):
            buf[c, :reach] = jnp.zeros((reach, width, LANES), jnp.float32)
            buf[c, reach + side :] = jnp.zeros((reach, width, LANES), jnp.float32)
            buf[c, reach : reach + side, :PAD] = jnp.zeros((side, PAD, LANES), jnp.float32)
            buf[c, reach : reach + side, PAD + side :] = jnp.zeros((side, PAD, LANES), jnp.float32)

    clear(xpad)
    clear(gpad)
    copies["owner"].wait()
    own = owner_ref[0, 0]
    table[me] = jnp.full((8, LANES), own, jnp.int32)

    def forward_conv(c):
        outs = depthwise(xpad, dww, c, taps, side, False)
        bias = vector(small[0], slice(c * LANES, (c + 1) * LANES))
        for parity in range(2):
            part = (outs[parity] + bias).reshape(half, 2, half, LANES)
            for row in range(2):
                sp[c, row * 2 + parity] = part[:, row].reshape(cells, LANES)

    copies[("s", 0)].wait()
    for c in range(chunks):
        copies[("w", c)].wait()
        copies[("x", c)].wait()
    forward_conv(0)

    across = 1 + (me > 0).astype(jnp.int32) + (me < peers - 1).astype(jnp.int32)
    along = (g > 0).astype(jnp.int32) + (g < groups - 1).astype(jnp.int32)
    pl.semaphore_wait(barrier, peers - 1 + across * along)

    def all_peers(src_of, dst_of, send, recv):
        moves = []
        for k in range(1, peers):
            moves.append(
                pltpu.make_async_remote_copy(
                    src_ref=src_of(k),
                    dst_ref=dst_of(k),
                    send_sem=send.at[k - 1],
                    recv_sem=recv.at[k - 1],
                    device_id={"group": g, "peer": lax.rem(me + k, peers)},
                    device_id_type=MESH,
                )
            )
        return moves

    table_moves = all_peers(lambda k: table.at[me], lambda k: table.at[me], tab_send, tab_recv)
    for move in table_moves:
        move.start()
    forward_conv(1)
    for move in table_moves:
        move.wait()
    copies["tg"].wait()

    def place_of(who):
        mine = table[who] == me
        before = jnp.zeros((8, LANES), jnp.int32)
        for p in range(peers):
            earlier = (p < who).astype(jnp.int32)
            before = before + jnp.where(table[p] == me, earlier, 0)
        return mine, before

    def wide(mask):
        return jnp.concatenate([mask.astype(jnp.float32)] * chunks, axis=1)

    def block_for(who):
        mine, before = place_of(who)
        total = None
        for s in range(slots):
            part = tg[s] * wide(jnp.logical_and(mine, before == s))
            total = part if total is None else total + part
        return total

    grad_moves = all_peers(lambda k: sendg.at[k - 1], lambda k: recvg.at[k - 1], g_send, g_recv)
    for k in range(1, peers):
        sendg[k - 1] = block_for(lax.rem(me + k, peers))
        grad_moves[k - 1].start()
    grid_g[1 : half + 1, PAD : PAD + half, :] = block_for(me)
    for c in range(2, chunks):
        forward_conv(c)

    for i in range(1, 6):
        copies[("s", i)].wait()
    for q in range(4):
        parts = [sp[c, q] for c in range(chunks)]
        mean = jnp.sum(functools.reduce(jnp.add, parts), axis=1, keepdims=True) / channels
        parts = [part - mean for part in parts]
        square = functools.reduce(jnp.add, [part * part for part in parts])
        inv = lax.rsqrt(jnp.sum(square, axis=1, keepdims=True) / channels + 1e-06)
        rstd[q] = jnp.broadcast_to(inv, (cells, LANES))
        for c in range(chunks):
            lane = slice(c * LANES, (c + 1) * LANES)
            hat = parts[c] * inv
            sp[c, q] = hat
            nb[q * cells : (q + 1) * cells, lane] = (
                hat * vector(small[1], lane) + vector(small[2], lane)
            ).astype(jnp.bfloat16)

    def halo_moves(grid, col, halo, send, recv):
        moves = []
        for i, (dr, dp) in enumerate(ROWS):
            if dr == 0:
                src = col.at[0 if dp < 0 else 1]
            else:
                src = grid.at[1 if dr < 0 else half, PAD : PAD + half, :]
            back = len(ROWS) - 1 - i
            moves.append(
                pltpu.make_async_remote_copy(
                    src_ref=src,
                    dst_ref=halo.at[back],
                    send_sem=send.at[i],
                    recv_sem=recv.at[back],
                    device_id={"group": g + dr, "peer": me + dp},
                    device_id_type=MESH,
                )
            )
        return moves

    def halo_start(grid, col, moves):
        col[0] = grid[1 : half + 1, PAD, :]
        col[1] = grid[1 : half + 1, PAD + half - 1, :]
        for (dr, dp), move in zip(ROWS, moves):

            @pl.when(there(dr, dp))
            def _():
                move.start()

    def halo_finish(grid, halo, moves, send, recv):
        for i, (dr, dp) in enumerate(ROWS):

            @pl.when(there(dr, dp))
            def _():
                moves[i].wait_send()
                pltpu.make_async_remote_copy(
                    src_ref=halo.at[i],
                    dst_ref=halo.at[i],
                    send_sem=send.at[i],
                    recv_sem=recv.at[i],
                    device_id={"group": g + dr, "peer": me + dp},
                    device_id_type=MESH,
                ).wait_recv()

        image = image_ref[g]
        keep = {
            -1: (image_ref[jnp.maximum(g - 1, 0)] == image).astype(jnp.float32) * (g > 0).astype(jnp.float32),
            0: 1.0,
            1: (image_ref[jnp.minimum(g + 1, groups - 1)] == image).astype(jnp.float32)
            * (g < groups - 1).astype(jnp.float32),
        }
        edge = {-1: (me > 0).astype(jnp.float32), 0: 1.0, 1: (me < peers - 1).astype(jnp.float32)}
        for i, (dr, dp) in enumerate(ROWS):
            row = {-1: 0, 1: half + 1}.get(dr)
            factor = keep[dr] * edge[dp]
            if dr == 0:
                grid[1 : half + 1, PAD - 1 if dp < 0 else PAD + half, :] = halo[i] * factor
            elif dp == 0:
                grid[row, PAD : PAD + half, :] = halo[i] * factor
            elif dp < 0:
                grid[row, PAD - 1 : PAD, :] = halo[i, half - 1 : half, :] * factor
            else:
                grid[row, PAD + half : PAD + half + 1, :] = halo[i, 0:1, :] * factor

    def window(grid, a, b):
        part = grid[a : a + half, PAD - 1 + b : PAD - 1 + b + half, :]
        return part.reshape(cells, channels).astype(jnp.bfloat16)

    g_moves = halo_moves(grid_g, col_g, halo_g, hg_send, hg_recv)
    p_moves = halo_moves(grid_p, col_p, halo_p, hp_send, hp_recv)

    def gather_grads():
        total = grid_g[1 : half + 1, PAD : PAD + half, :]
        for k in range(1, peers):
            grad_moves[k - 1].wait()
            total = total + recvg[k - 1]
        grid_g[1 : half + 1, PAD : PAD + half, :] = total
        halo_start(grid_g, col_g, g_moves)

    copies["bin"].wait()
    copies["image"].wait()
    copies["win"].wait()
    for n in range(hid // BLOCK):
        lane = slice(n * BLOCK, (n + 1) * BLOCK)
        pre_all = jnp.dot(nb[...], win[:, lane], preferred_element_type=jnp.float32)
        bias = vector(bin_, lane)
        pooled = None
        for q in range(4):
            pre = pre_all[q * cells : (q + 1) * cells] + bias
            cdf = 0.5 + 0.5 * lax.erf(pre * math.sqrt(0.5))
            pdf = jnp.exp(pre * pre * -0.5) * (1.0 / math.sqrt(2.0 * math.pi))
            dg[q * cells : (q + 1) * cells, lane] = cdf + pre * pdf
            value = pre * cdf
            pooled = value if pooled is None else pooled + value
        hb[:, lane] = (pooled * 0.25).astype(jnp.bfloat16)
        if n == hid // BLOCK - 2:
            gather_grads()
    copies["wout"].wait()
    branch = jnp.dot(hb[...], wout[...], preferred_element_type=jnp.float32)
    for c in range(chunks):
        lane = slice(c * LANES, (c + 1) * LANES)
        total = None
        for row in range(2):
            for parity in range(2):
                part = xpad[c, reach : reach + side, pl.ds(PAD + parity, half, stride=2), :]
                part = part.reshape(half, 2, half, LANES)[:, row]
                total = part if total is None else total + part
        mixed = vector(small[4], lane) * (branch[:, lane] + vector(small[3], lane))
        grid_p[1 : half + 1, PAD : PAD + half, lane] = total * 0.25 + mixed.reshape(half, half, LANES)
    halo_start(grid_p, col_p, p_moves)

    copies["cw"].wait()
    halo_finish(grid_g, halo_g, g_moves, hg_send, hg_recv)
    grads = None
    for a in range(3):
        for b in range(3):
            part = nt_dot(window(grid_g, a, b), cw[(2 - a) * 3 + 2 - b])
            grads = part if grads is None else grads + part
    grads = grads * 0.25
    for c in range(chunks):
        lane = slice(c * LANES, (c + 1) * LANES)
        gq[c] = grads[:, lane].reshape(half, half, LANES)
    scaled = (grads * vector(scale)).astype(jnp.bfloat16)

    halo_finish(grid_p, halo_p, p_moves, hp_send, hp_recv)
    comp = None
    for a in range(3):
        for b in range(3):
            part = jnp.dot(window(grid_p, a, b), cw[a * 3 + b], preferred_element_type=jnp.float32)
            comp = part if comp is None else comp + part
    tok[...] = (comp + vector(cb)).reshape(half, half, channels)
    tok_moves = all_peers(lambda k: tok, lambda k: recvt.at[k - 1], t_send, t_recv)
    for move in tok_moves:
        move.start()

    for n in range(hid // BLOCK):
        lane = slice(n * BLOCK, (n + 1) * BLOCK)
        dh = nt_dot(scaled, wout[lane, :])
        for q in range(4):
            rows = slice(q * cells, (q + 1) * cells)
            dpb[rows, lane] = (dh * dg[rows, lane]).astype(jnp.bfloat16)
    for q in range(4):
        dn = nt_dot(dpb[q * cells : (q + 1) * cells, :], win[...]) * vector(gain)
        parts = [dn[:, c * LANES : (c + 1) * LANES] for c in range(chunks)]
        first = jnp.sum(functools.reduce(jnp.add, parts), axis=1, keepdims=True) / channels
        cross = functools.reduce(jnp.add, [parts[c] * sp[c, q] for c in range(chunks)])
        second = jnp.sum(cross, axis=1, keepdims=True) / channels
        for c in range(chunks):
            back = rstd[q] * (parts[c] - first - sp[c, q] * second)
            back = back.reshape(half, half, LANES)
            for i in range(half):
                gpad[c, reach + 2 * i + q // 2, pl.ds(PAD + q % 2, half, stride=2), :] = back[i]

    out_copies = []
    for c in range(chunks):
        outs = depthwise(gpad, dww, c, taps, side, True)
        direct = jnp.broadcast_to(gq[c][:, None], (half, 2, half, LANES)).reshape(side, half, LANES)
        for parity in range(2):
            value = outs[parity] + direct
            for i in range(side):
                obuf[c, i, pl.ds(parity, half, stride=2), :] = value[i]
        copy = pltpu.make_async_copy(
            obuf.at[c], dx_hbm.at[:, :, c * LANES : (c + 1) * LANES], out_sems.at[c]
        )
        copy.start()
        out_copies.append(copy)

    for move in tok_moves:
        move.wait()
    mine, before = place_of(me)
    outs = [tok[...] * wide(jnp.logical_and(mine, before == s)) for s in range(slots)]
    for k in range(1, peers):
        mine, before = place_of(lax.rem(me + peers - k, peers))
        for s in range(slots):
            outs[s] = outs[s] + recvt[k - 1] * wide(jnp.logical_and(mine, before == s))
    for s in range(slots):
        tokout[s] = outs[s]
    copy = pltpu.make_async_copy(tokout, tok_hbm, out_sems.at[chunks])
    copy.start()
    copy.wait()
    for copy in out_copies:
        copy.wait()


def solution(mesh):
    groups, peers = mesh.shape["group"], mesh.shape["peer"]

    def on_device(
        features, image_of_row, llm_peer, token_grads, dw_weight, dw_bias, ln_gain, ln_bias,
        w_in, b_in, w_out, b_out, layer_scale, comp_weight, comp_bias,
    ):
        side, width, channels = features.shape
        slots = token_grads.shape[0]
        hid = w_in.shape[1]
        taps = math.isqrt(dw_weight.shape[0])
        half = side // 2
        cells = half * half
        chunks = channels // LANES
        assert width == side and llm_peer.shape == (1, 1)
        f32, bf16 = jnp.float32, jnp.bfloat16
        padded = (chunks, side + 2 * (taps // 2), side + 2 * PAD, LANES)
        grid = (half + 2, half + 2 * PAD, channels)
        block = (half, half, channels)
        dma = pltpu.SemaphoreType.DMA
        hbm = pl.BlockSpec(memory_space=pl.ANY)
        tokens, grads = pl.pallas_call(
            functools.partial(kernel, groups, peers, taps),
            out_shape=(
                jax.ShapeDtypeStruct((slots,) + block, f32),
                jax.ShapeDtypeStruct(features.shape, f32),
            ),
            in_specs=[hbm] * 15,
            out_specs=(hbm, hbm),
            scratch_shapes=[
                pltpu.VMEM(padded, f32),
                pltpu.VMEM(padded, f32),
                pltpu.VMEM((chunks, taps * taps, LANES), f32),
                *[pltpu.VMEM((channels,), f32)] * 6,
                pltpu.VMEM((hid,), f32),
                pltpu.VMEM(w_in.shape, bf16),
                pltpu.VMEM(w_out.shape, bf16),
                pltpu.VMEM(comp_weight.shape, bf16),
                pltpu.VMEM((slots,) + block, f32),
                pltpu.VMEM((chunks, 4, cells, LANES), f32),
                pltpu.VMEM((4, cells, LANES), f32),
                pltpu.VMEM((4 * cells, channels), bf16),
                pltpu.VMEM((4 * cells, hid), f32),
                pltpu.VMEM((cells, hid), bf16),
                pltpu.VMEM((4 * cells, hid), bf16),
                pltpu.VMEM((peers, 8, LANES), jnp.int32),
                pltpu.VMEM((peers - 1,) + block, f32),
                pltpu.VMEM((peers - 1,) + block, f32),
                pltpu.VMEM(block, f32),
                pltpu.VMEM((peers - 1,) + block, f32),
                pltpu.VMEM((slots,) + block, f32),
                pltpu.VMEM(grid, f32),
                pltpu.VMEM(grid, f32),
                pltpu.VMEM((2, half, channels), f32),
                pltpu.VMEM((2, half, channels), f32),
                pltpu.VMEM((8, half, channels), f32),
                pltpu.VMEM((8, half, channels), f32),
                pltpu.VMEM((chunks, half, half, LANES), f32),
                pltpu.VMEM((chunks, side, side, LANES), f32),
                pltpu.SMEM(image_of_row.shape, jnp.int32),
                pltpu.SMEM((1, 1), jnp.int32),
                dma((2 * chunks + 13,)),
                dma((chunks + 1,)),
                dma((peers - 1,)),
                dma((peers - 1,)),
                dma((peers - 1,)),
                dma((peers - 1,)),
                dma((peers - 1,)),
                dma((peers - 1,)),
                dma((8,)),
                dma((8,)),
                dma((8,)),
                dma((8,)),
            ],
            compiler_params=pltpu.CompilerParams(collective_id=0, has_side_effects=True),
        )(
            image_of_row,
            llm_peer,
            features,
            token_grads.reshape((slots,) + block),
            dw_weight,
            dw_bias,
            ln_gain,
            ln_bias,
            w_in,
            b_in,
            w_out,
            b_out,
            layer_scale,
            comp_weight,
            comp_bias,
        )
        return tokens.reshape(slots, cells, channels), grads

    placed = [P()] * 15
    placed[0] = P("group", "peer", None)
    placed[2] = P(("group", "peer"), None)
    placed[3] = P(("group", "peer"), None, None)
    return jax.shard_map(
        on_device,
        mesh=mesh,
        in_specs=tuple(placed),
        out_specs=(P(("group", "peer"), None, None), P("group", "peer", None)),
        check_vma=False,
    )
```

time: 117 us -> 29.2 us (0.25)
  other arithmetic: 36.2 us -> 0 us
  starting transfers between devices: 33.1 us -> 0 us
  Pallas kernels: 0 us -> 24.3 us
  matrix products: 18.7 us -> 0 us
  local copies, waits for them, and re-layouts: 16 us -> 3.38 us
  blocking collectives: 4.82 us -> 0 us
  between operations: 4.37 us -> 1.29 us
  waiting for transfers between devices: 2.86 us -> 0 us
    pallas_call x0 -> x1, Pallas kernels: none -> 24.3 us  [on_device(): pl.pallas_call(functools.partial(kernel, groups, peers, taps), out_shape=...]
    ppermute x8 -> x0, starting transfers between devices: 24.3 us -> none  [the longest x4 13.3 us: with_halo(): lax.ppermute(tail, axis, [(i, (i + 1) % count) for i in range(ends)])]
    dot_general x24 -> x0, matrix products: 18.7 us -> none  [the longest x2 7.78 us: encode(): jnp.dot(flattened, w_in, preferred_element_type=jnp.float32) + b_in]
    reduce_sum x5 -> x0, other arithmetic: 16 us -> none  [the longest x1 15.1 us: encode(): average = jnp.mean(spatial, axis=-1, keepdims=True)]
    mul x6 -> x0, other arithmetic: 8.89 us -> none  [the longest x4 8.87 us: encode(): padded[:, row_off:row_off + tile_side, col_off:col_off + tile_side, :]]
    all_to_all x2 -> x0, starting transfers between devices: 8.87 us -> none  [the longest x1 4.78 us: on_device(): lax.all_to_all(spread_back, 'peer', split_axis=0, concat_axis=0, tiled=True)]
    add_any x1 -> x0, other arithmetic: 7.57 us -> none  [encode(): padded[:, row_off:row_off + tile_side, col_off:col_off + tile_side, :]]
    unnamed x1 -> x0, blocking collectives: 4.82 us -> none
  transfers between devices with their start and end apart: 10 -> 0, of which waited for: 1 -> 0; matrix products, arithmetic and copies ran while one was open for 18% -> 0% of each run, Pallas kernels for 0% -> 0%
where the time goes in v1:
time: 29.2 us; the launch traced here: 29 us
  Pallas kernels  24.3 us (83%)
  local copies, waits for them, and re-layouts  3.38 us (12%)
  between operations  1.29 us (4%)
    pallas_call x1, Pallas kernels, on_device(): pl.pallas_call(functools.partial(kernel, groups, peers, taps), out_shape=...  24.3 us
    unnamed x2, local copies, waits for them, and re-layouts  3.38 us

profile of v1, /device:TPU:25, one launch (start us, length us, event | category | flops | bytes accessed | tf_op | source)
XLA Modules:
  0.0 29.0 jit_solution(7555241326252689419)
XLA Ops:
  1.3 24.3 %shard_map.158 = (f32[2,8,8,384]{3,2,1,0:T(8,128)}, f32[16,16,384]{2,1,0:T(8,128)}) custom-call(s32[8]{0:T(128)} %image_hbm.1, s32[1,1]{1,0:T(1,128)S(6)} %copy.19.owner_hbm, f32[16,16,384]{2,1,0:T(8,128)} %x_hbm.1, f32[2,8,8,384]{3,2,1,0:T(8,128)} %bitcast.2, f32[49,384]{1,0:T(8,128)} %dww_hbm.1, f32[384]{0:T(512)} %dwb_hbm.1, f32[384]{0:T(512)} %gain_hbm.1, ...), custom_call_target="tpu_custom_call" | custom-call | tf_op jit(solution)/shard_map/pallas_call | solution.py:480
  25.6 1.6 %copy.20 = f32[2,64,384]{2,1,0:T(8,128)} copy(f32[2,64,384]{2,1,0:T(8,128)} %bitcast.3) | data formatting | bytes 393216
  27.2 1.8 %copy.21 = f32[16,16,384]{2,1,0:T(8,128)} copy(f32[16,16,384]{2,1,0:T(8,128)} %get-tuple-element.9) | data formatting | bytes 786432

commit v2 on v1

--- a/solution.py
+++ b/solution.py
@@ -54,11 +54,11 @@
     scale_hbm,
     cw_hbm,
     cb_hbm,
-    tok_hbm,
-    dx_hbm,
-    xpad,
     gpad,
     dww,
+    gq,
+    tokout,
+    xpad,
     dwb,
     gain,
     lnb,
@@ -79,27 +79,30 @@
     table,
     sendg,
     recvg,
+    sendf,
+    recvf,
     tok,
     recvt,
-    tokout,
+    recvr,
     grid_g,
     grid_p,
     col_g,
     col_p,
     halo_g,
     halo_p,
-    gq,
-    obuf,
     image_ref,
     owner_ref,
     in_sems,
-    out_sems,
     tab_send,
     tab_recv,
+    near_send,
+    near_recv,
     g_send,
     g_recv,
     t_send,
     t_recv,
+    r_send,
+    r_recv,
     hg_send,
     hg_recv,
     hp_send,
@@ -195,35 +198,28 @@
             for row in range(2):
                 sp[c, row * 2 + parity] = part[:, row].reshape(cells, LANES)
 
+    across = 1 + (me > 0).astype(jnp.int32) + (me < peers - 1).astype(jnp.int32)
+    along = (g > 0).astype(jnp.int32) + (g < groups - 1).astype(jnp.int32)
+    pl.semaphore_wait(barrier, peers - 1 + across * along)
+
+    table_moves = []
+    for k in range(1, peers):
+        table_moves.append(
+            pltpu.make_async_remote_copy(
+                src_ref=table.at[me],
+                dst_ref=table.at[me],
+                send_sem=tab_send.at[k - 1],
+                recv_sem=tab_recv.at[k - 1],
+                device_id={"group": g, "peer": lax.rem(me + k, peers)},
+                device_id_type=MESH,
+            )
+        )
+        table_moves[-1].start()
     copies[("s", 0)].wait()
     for c in range(chunks):
         copies[("w", c)].wait()
         copies[("x", c)].wait()
-    forward_conv(0)
-
-    across = 1 + (me > 0).astype(jnp.int32) + (me < peers - 1).astype(jnp.int32)
-    along = (g > 0).astype(jnp.int32) + (g < groups - 1).astype(jnp.int32)
-    pl.semaphore_wait(barrier, peers - 1 + across * along)
-
-    def all_peers(src_of, dst_of, send, recv):
-        moves = []
-        for k in range(1, peers):
-            moves.append(
-                pltpu.make_async_remote_copy(
-                    src_ref=src_of(k),
-                    dst_ref=dst_of(k),
-                    send_sem=send.at[k - 1],
-                    recv_sem=recv.at[k - 1],
-                    device_id={"group": g, "peer": lax.rem(me + k, peers)},
-                    device_id_type=MESH,
-                )
-            )
-        return moves
-
-    table_moves = all_peers(lambda k: table.at[me], lambda k: table.at[me], tab_send, tab_recv)
-    for move in table_moves:
-        move.start()
-    forward_conv(1)
+        forward_conv(c)
     for move in table_moves:
         move.wait()
     copies["tg"].wait()
@@ -247,13 +243,38 @@
             total = part if total is None else total + part
         return total
 
-    grad_moves = all_peers(lambda k: sendg.at[k - 1], lambda k: recvg.at[k - 1], g_send, g_recv)
-    for k in range(1, peers):
-        sendg[k - 1] = block_for(lax.rem(me + k, peers))
-        grad_moves[k - 1].start()
+    pairs = peers // 2
+    core = lax.rem(me, 2)
+    partner = me + 1 - 2 * core
+
+    def seat(k, which):
+        return lax.rem(lax.div(me, 2) + k, pairs) * 2 + which
+
+    def to(src, dst, send, recv, where):
+        return pltpu.make_async_remote_copy(
+            src_ref=src,
+            dst_ref=dst,
+            send_sem=send,
+            recv_sem=recv,
+            device_id={"group": g, "peer": where},
+            device_id_type=MESH,
+        )
+
+    for k in range(pairs):
+        sendg[k] = block_for(seat(k, 1 - core))
+    near_move = to(sendg, recvg, near_send, near_recv, partner)
+    near_move.start()
     grid_g[1 : half + 1, PAD : PAD + half, :] = block_for(me)
-    for c in range(2, chunks):
-        forward_conv(c)
+    far_moves = [
+        to(sendf.at[k - 1], recvf.at[k - 1], g_send.at[k - 1], g_recv.at[k - 1], seat(k, core))
+        for k in range(1, pairs)
+    ]
+
+    def pass_on():
+        near_move.wait()
+        for k in range(1, pairs):
+            sendf[k - 1] = block_for(seat(k, core)) + recvg[k]
+            far_moves[k - 1].start()
 
     for i in range(1, 6):
         copies[("s", i)].wait()
@@ -344,10 +365,10 @@
     p_moves = halo_moves(grid_p, col_p, halo_p, hp_send, hp_recv)
 
     def gather_grads():
-        total = grid_g[1 : half + 1, PAD : PAD + half, :]
-        for k in range(1, peers):
-            grad_moves[k - 1].wait()
-            total = total + recvg[k - 1]
+        total = grid_g[1 : half + 1, PAD : PAD + half, :] + recvg[0]
+        for k in range(1, pairs):
+            far_moves[k - 1].wait()
+            total = total + recvf[k - 1]
         grid_g[1 : half + 1, PAD : PAD + half, :] = total
         halo_start(grid_g, col_g, g_moves)
 
@@ -368,7 +389,7 @@
             pooled = value if pooled is None else pooled + value
         hb[:, lane] = (pooled * 0.25).astype(jnp.bfloat16)
         if n == hid // BLOCK - 2:
-            gather_grads()
+            pass_on()
     copies["wout"].wait()
     branch = jnp.dot(hb[...], wout[...], preferred_element_type=jnp.float32)
     for c in range(chunks):
@@ -384,6 +405,20 @@
     halo_start(grid_p, col_p, p_moves)
 
     copies["cw"].wait()
+    halo_finish(grid_p, halo_p, p_moves, hp_send, hp_recv)
+    comp = None
+    for a in range(3):
+        for b in range(3):
+            part = jnp.dot(window(grid_p, a, b), cw[a * 3 + b], preferred_element_type=jnp.float32)
+            comp = part if comp is None else comp + part
+    tok[...] = (comp + vector(cb)).reshape(half, half, channels)
+    tok_moves = [to(tok, recvt.at[0], t_send.at[0], t_recv.at[0], partner)]
+    for k in range(1, pairs):
+        tok_moves.append(to(tok, recvt.at[k], t_send.at[k], t_recv.at[k], seat(k, core)))
+    for move in reversed(tok_moves):
+        move.start()
+    gather_grads()
+
     halo_finish(grid_g, halo_g, g_moves, hg_send, hg_recv)
     grads = None
     for a in range(3):
@@ -396,16 +431,13 @@
         gq[c] = grads[:, lane].reshape(half, half, LANES)
     scaled = (grads * vector(scale)).astype(jnp.bfloat16)
 
-    halo_finish(grid_p, halo_p, p_moves, hp_send, hp_recv)
-    comp = None
-    for a in range(3):
-        for b in range(3):
-            part = jnp.dot(window(grid_p, a, b), cw[a * 3 + b], preferred_element_type=jnp.float32)
-            comp = part if comp is None else comp + part
-    tok[...] = (comp + vector(cb)).reshape(half, half, channels)
-    tok_moves = all_peers(lambda k: tok, lambda k: recvt.at[k - 1], t_send, t_recv)
-    for move in tok_moves:
-        move.start()
+    relays = []
+
+    def relay():
+        for k in range(1, pairs):
+            tok_moves[k].wait()
+            relays.append(to(recvt.at[k], recvr.at[k - 1], r_send.at[k - 1], r_recv.at[k - 1], partner))
+            relays[-1].start()
 
     for n in range(hid // BLOCK):
         lane = slice(n * BLOCK, (n + 1) * BLOCK)
@@ -413,6 +445,7 @@
         for q in range(4):
             rows = slice(q * cells, (q + 1) * cells)
             dpb[rows, lane] = (dh * dg[rows, lane]).astype(jnp.bfloat16)
+    relay()
     for q in range(4):
         dn = nt_dot(dpb[q * cells : (q + 1) * cells, :], win[...]) * vector(gain)
         parts = [dn[:, c * LANES : (c + 1) * LANES] for c in range(chunks)]
@@ -425,7 +458,29 @@
             for i in range(half):
                 gpad[c, reach + 2 * i + q // 2, pl.ds(PAD + q % 2, half, stride=2), :] = back[i]
 
-    out_copies = []
+    tok_moves[0].wait()
+    for move in relays:
+        move.wait()
+    arrived = [(me, tok), (partner, recvt.at[0])]
+    for k in range(1, pairs):
+        arrived.append((seat(pairs - k, core), recvt.at[k]))
+        arrived.append((seat(pairs - k, 1 - core), recvr.at[k - 1]))
+    outs = [None] * slots
+    for who, block in arrived:
+        mine, before = place_of(who)
+        for s in range(slots):
+            part = block[...] * wide(jnp.logical_and(mine, before == s))
+            outs[s] = part if outs[s] is None else outs[s] + part
+    for s in range(slots):
+        tokout[s] = outs[s]
+
+
+def tail(taps, gpad, dww, gq, tokout, tok_hbm, dx_hbm, obuf, sems):
+    chunks = gpad.shape[0]
+    side = dx_hbm.shape[0]
+    half = side // 2
+    copies = [pltpu.make_async_copy(tokout, tok_hbm, sems.at[chunks])]
+    copies[0].start()
     for c in range(chunks):
         outs = depthwise(gpad, dww, c, taps, side, True)
         direct = jnp.broadcast_to(gq[c][:, None], (half, 2, half, LANES)).reshape(side, half, LANES)
@@ -434,25 +489,11 @@
             for i in range(side):
                 obuf[c, i, pl.ds(parity, half, stride=2), :] = value[i]
         copy = pltpu.make_async_copy(
-            obuf.at[c], dx_hbm.at[:, :, c * LANES : (c + 1) * LANES], out_sems.at[c]
+            obuf.at[c], dx_hbm.at[:, :, c * LANES : (c + 1) * LANES], sems.at[c]
         )
         copy.start()
-        out_copies.append(copy)
-
-    for move in tok_moves:
-        move.wait()
-    mine, before = place_of(me)
-    outs = [tok[...] * wide(jnp.logical_and(mine, before == s)) for s in range(slots)]
-    for k in range(1, peers):
-        mine, before = place_of(lax.rem(me + peers - k, peers))
-        for s in range(slots):
-            outs[s] = outs[s] + recvt[k - 1] * wide(jnp.logical_and(mine, before == s))
-    for s in range(slots):
-        tokout[s] = outs[s]
-    copy = pltpu.make_async_copy(tokout, tok_hbm, out_sems.at[chunks])
-    copy.start()
-    copy.wait()
-    for copy in out_copies:
+        copies.append(copy)
+    for copy in copies:
         copy.wait()
 
 
@@ -476,19 +517,23 @@
         grid = (half + 2, half + 2 * PAD, channels)
         block = (half, half, channels)
         dma = pltpu.SemaphoreType.DMA
-        hbm = pl.BlockSpec(memory_space=pl.ANY)
-        tokens, grads = pl.pallas_call(
+        hbm = pl.BlockSpec(memory_space=pltpu.HBM)
+        pairs = peers // 2
+        assert peers == 2 * pairs and pairs > 1
+        vmem = pl.BlockSpec(memory_space=pltpu.VMEM)
+        held = (
+            pltpu.VMEM(padded, f32),
+            pltpu.VMEM((chunks, taps * taps, LANES), f32),
+            pltpu.VMEM((chunks, half, half, LANES), f32),
+            pltpu.VMEM((slots,) + block, f32),
+        )
+        state = pl.pallas_call(
             functools.partial(kernel, groups, peers, taps),
-            out_shape=(
-                jax.ShapeDtypeStruct((slots,) + block, f32),
-                jax.ShapeDtypeStruct(features.shape, f32),
-            ),
+            out_shape=held,
             in_specs=[hbm] * 15,
-            out_specs=(hbm, hbm),
+            out_specs=(vmem,) * 4,
             scratch_shapes=[
                 pltpu.VMEM(padded, f32),
-                pltpu.VMEM(padded, f32),
-                pltpu.VMEM((chunks, taps * taps, LANES), f32),
                 *[pltpu.VMEM((channels,), f32)] * 6,
                 pltpu.VMEM((hid,), f32),
                 pltpu.VMEM(w_in.shape, bf16),
@@ -502,29 +547,32 @@
                 pltpu.VMEM((cells, hid), bf16),
                 pltpu.VMEM((4 * cells, hid), bf16),
                 pltpu.VMEM((peers, 8, LANES), jnp.int32),
-                pltpu.VMEM((peers - 1,) + block, f32),
-                pltpu.VMEM((peers - 1,) + block, f32),
+                pltpu.VMEM((pairs,) + block, f32),
+                pltpu.VMEM((pairs,) + block, f32),
+                pltpu.VMEM((pairs - 1,) + block, f32),
+                pltpu.VMEM((pairs - 1,) + block, f32),
                 pltpu.VMEM(block, f32),
-                pltpu.VMEM((peers - 1,) + block, f32),
-                pltpu.VMEM((slots,) + block, f32),
+                pltpu.VMEM((pairs,) + block, f32),
+                pltpu.VMEM((pairs - 1,) + block, f32),
                 pltpu.VMEM(grid, f32),
                 pltpu.VMEM(grid, f32),
                 pltpu.VMEM((2, half, channels), f32),
                 pltpu.VMEM((2, half, channels), f32),
                 pltpu.VMEM((8, half, channels), f32),
                 pltpu.VMEM((8, half, channels), f32),
-                pltpu.VMEM((chunks, half, half, LANES), f32),
-                pltpu.VMEM((chunks, side, side, LANES), f32),
                 pltpu.SMEM(image_of_row.shape, jnp.int32),
                 pltpu.SMEM((1, 1), jnp.int32),
                 dma((2 * chunks + 13,)),
-                dma((chunks + 1,)),
                 dma((peers - 1,)),
                 dma((peers - 1,)),
-                dma((peers - 1,)),
-                dma((peers - 1,)),
-                dma((peers - 1,)),
-                dma((peers - 1,)),
+                dma,
+                dma,
+                dma((pairs - 1,)),
+                dma((pairs - 1,)),
+                dma((pairs,)),
+                dma((pairs,)),
+                dma((pairs - 1,)),
+                dma((pairs - 1,)),
                 dma((8,)),
                 dma((8,)),
                 dma((8,)),
@@ -548,6 +596,17 @@
             comp_weight,
             comp_bias,
         )
+        tokens, grads = pl.pallas_call(
+            functools.partial(tail, taps),
+            out_shape=(
+                jax.ShapeDtypeStruct((slots,) + block, f32),
+                jax.ShapeDtypeStruct(features.shape, f32),
+            ),
+            in_specs=[vmem] * 4,
+            out_specs=(hbm, hbm),
+            scratch_shapes=[pltpu.VMEM((chunks, side, side, LANES), f32), dma((chunks + 1,))],
+            compiler_params=pltpu.CompilerParams(vmem_limit_bytes=16 << 20),
+        )(*state)
         return tokens.reshape(slots, cells, channels), grads
 
     placed = [P()] * 15

time: 29.2 us -> 24.6 us (0.84)
  the two profiles are of different devices: /device:TPU:25 before, /device:TPU:1 now
where the time goes in v2:
time: 24.6 us; the launch traced here: 24.5 us
  Pallas kernels  23.2 us (94%)
  between operations  1.29 us (5%)
    pallas_call x1, Pallas kernels, on_device(): pl.pallas_call(functools.partial(kernel, groups, peers, taps), out_shape=...  20.9 us
    pallas_call x1, Pallas kernels, on_device(): pl.pallas_call(functools.partial(tail, taps), out_shape=(jax.ShapeDtypeSt...  2.32 us

profile of v2, /device:TPU:1, one launch (start us, length us, event | category | flops | bytes accessed | tf_op | source)
XLA Modules:
  0.0 24.5 jit_solution(16038661313562220491)
XLA Ops:
  1.3 20.9 %shard_map.158 = (f32[3,22,32,128]{3,2,1,0:T(8,128)S(1)}, f32[3,49,128]{2,1,0:T(8,128)S(1)}, f32[3,8,8,128]{3,2,1,0:T(8,128)S(1)}, f32[2,8,8,384]{3,2,1,0:T(8,128)S(1)}) custom-call(s32[8]{0:T(128)} %image_hbm.1, s32[1,1]{1,0:T(1,128)S(6)} %copy.17.owner_hbm, f32[16,16,384]{2,1,0:T(8,128)} %x_hbm.1, f32[2,8,8,384]{3,2,1,0:T(8,128)} %bitcast.2, ...), custom_call_target="tpu_custom_call" | custom-call | tf_op jit(solution)/shard_map/pallas_call | solution.py:530
  22.1 2.3 %shard_map.159 = (f32[2,8,8,384]{3,2,1,0:T(8,128)}, f32[16,16,384]{2,1,0:T(8,128)}) custom-call(f32[3,22,32,128]{3,2,1,0:T(8,128)S(1)} %get-tuple-element.8.gpad, f32[3,49,128]{2,1,0:T(8,128)S(1)} %get-tuple-element.9.dww, f32[3,8,8,128]{3,2,1,0:T(8,128)S(1)} %get-tuple-element.10.gq, f32[2,8,8,384]{3,2,1,0:T(8,128)S(1)} %get-tuple-element.11.tokout), custom_call_target="tpu_custom_call" | custom-call | tf_op jit(solution)/shard_map/pallas_call | solution.py:599
